TPU v7x, 32 devices: a whole 2x2x4 slice. The times are simulated.
32 devices in a mesh: ctx: 8 (over y, x, core), fsdp: 4 (over z).
Axes of the slice: x: 2, y: 2, z: 4, core: 2. Of those that a mesh axis runs over, the one named last changes fastest.
Arguments:
- tokens: bfloat16 [4096, 1600], P(('fsdp', 'ctx')), may hold values from -6 to 6
- block_table: int32 [8, 2], replicated, may hold values from 0 to 15, as said below
- ln1_gain: bfloat16 [1600], P('fsdp'), may hold values from 0.099609375 to 1.8984375
- ln1_bias: bfloat16 [1600], P('fsdp'), may hold values from -1.75 to 1.75
- qkv_weight: bfloat16 [1600, 4800], P('fsdp'), may hold values from -0.15625 to 0.15625
- query_bias: bfloat16 [1600], P('fsdp'), may hold values from -3 to 3
- value_bias: bfloat16 [1600], P('fsdp'), may hold values from -0.875 to 0.875
- proj_weight: bfloat16 [1600, 1600], P('fsdp'), may hold values from -1.25 to 1.25
- proj_bias: bfloat16 [1600], P('fsdp'), may hold values from -1.75 to 1.75
- ln2_gain: bfloat16 [1600], P('fsdp'), may hold values from 0.099609375 to 1.8984375
- ln2_bias: bfloat16 [1600], P('fsdp'), may hold values from -1.75 to 1.75
- fc_weight: bfloat16 [1600, 6400], P('fsdp'), may hold values from -0.15625 to 0.15625
- fc_bias: bfloat16 [6400], P('fsdp'), may hold values from -3 to 3
- out_weight: bfloat16 [6400, 1600], P('fsdp'), may hold values from -0.078125 to 0.078125
- out_bias: bfloat16 [1600], P('fsdp'), may hold values from -1.75 to 1.75
- cotangent: bfloat16 [4096, 1600], P(('fsdp', 'ctx')), may hold values from -6 to 6
Outputs:
- layer_out: bfloat16 [4096, 1600], P(('fsdp', 'ctx'))
- grad_tokens: bfloat16 [4096, 1600], P(('fsdp', 'ctx'))
- grad_ln1_gain: float32 [1600], P('fsdp')
- grad_ln1_bias: float32 [1600], P('fsdp')
- grad_qkv_weight: float32 [1600, 4800], P('fsdp')
- grad_query_bias: float32 [1600], P('fsdp')
- grad_value_bias: float32 [1600], P('fsdp')
- grad_proj_weight: float32 [1600, 1600], P('fsdp')
- grad_proj_bias: float32 [1600], P('fsdp')
- grad_ln2_gain: float32 [1600], P('fsdp')
- grad_ln2_bias: float32 [1600], P('fsdp')
- grad_fc_weight: float32 [1600, 6400], P('fsdp')
- grad_fc_bias: float32 [6400], P('fsdp')
- grad_out_weight: float32 [6400, 1600], P('fsdp')
- grad_out_bias: float32 [1600], P('fsdp')
Inputs may be any that keep to these rules, and one draw needn't show every extreme that they name: `block_table`: row i is (p_i, 15 - p_i) with p_i below 8; every block number appears exactly once.
All inputs are finite; a program needn't handle non-finite values.
Results may differ from a plain program's by a relative error of at most 0.02.
Values may be sent and summed in bfloat16 or wider, within the bound.
A program may use at most 256 MiB of HBM per device.

v0:
```python
import math
import jax
import jax.numpy as jnp
from jax import lax
from jax.sharding import PartitionSpec as P

HEADS = 25


def layer_norm(values, gain_vec, shift_vec):
    centre = values - jnp.mean(values, axis=-1, keepdims=True)
    spread = jnp.mean(centre * centre, axis=-1, keepdims=True)
    return centre * lax.rsqrt(spread + 1e-05) * gain_vec + shift_vec


def gelu_tanh(values):
    return jax.nn.gelu(values, approximate=True)


def body(
    tokens,
    block_table,
    ln1_gain,
    ln1_bias,
    qkv_weight,
    query_bias,
    value_bias,
    proj_weight,
    proj_bias,
    ln2_gain,
    ln2_bias,
    fc_weight,
    fc_bias,
    out_weight,
    out_bias,
    cotangent,
):
    row_count = tokens.shape[0]
    model_width = tokens.shape[1]
    block_rows = row_count // 2
    head_dim = model_width // HEADS
    score_scale = head_dim ** (-0.5)
    ctx_index = lax.axis_index("ctx")
    own_blocks = lax.dynamic_slice_in_dim(block_table, ctx_index, 1, 0).reshape(-1)
    offsets = jnp.arange(block_rows, dtype=jnp.int32)
    query_pos = (own_blocks[:, None] * block_rows + offsets[None, :]).reshape(-1)
    key_pos = (block_table.reshape(-1)[:, None] * block_rows + offsets[None, :]).reshape(-1)
    seq_len = key_pos.shape[0]
    key_block = math.gcd(seq_len, 512)
    block_count = seq_len // key_block
    pos_blocks = key_pos.reshape(block_count, key_block)
    gain_one, shift_one, qkv_full, q_bias, v_bias, proj_full, proj_b = (
        lax.all_gather(ln1_gain, "fsdp", axis=0, tiled=True),
        lax.all_gather(ln1_bias, "fsdp", axis=0, tiled=True),
        lax.all_gather(qkv_weight, "fsdp", axis=0, tiled=True),
        lax.all_gather(query_bias, "fsdp", axis=0, tiled=True),
        lax.all_gather(value_bias, "fsdp", axis=0, tiled=True),
        lax.all_gather(proj_weight, "fsdp", axis=0, tiled=True),
        lax.all_gather(proj_bias, "fsdp", axis=0, tiled=True),
    )
    inputs = tokens.astype(jnp.float32)
    gain_one_f = gain_one.astype(jnp.float32)
    shift_one_f = shift_one.astype(jnp.float32)
    normed_one = layer_norm(inputs, gain_one_f, shift_one_f).astype(jnp.bfloat16)
    bias_row = jnp.concatenate([q_bias, jnp.zeros_like(q_bias), v_bias]).astype(jnp.float32)
    joined = jnp.dot(normed_one, qkv_full, preferred_element_type=jnp.float32) + bias_row
    query_rows = joined[:, :model_width].astype(jnp.bfloat16).reshape(row_count, HEADS, head_dim)
    key_local = joined[:, model_width : 2 * model_width].astype(jnp.bfloat16)
    value_local = joined[:, 2 * model_width :].astype(jnp.bfloat16)
    key_all, value_all = (
        lax.all_gather(key_local, "ctx", axis=0, tiled=True),
        lax.all_gather(value_local, "ctx", axis=0, tiled=True),
    )

    def scores_of(key_tile, pos_tile):
        raw_scores = jnp.einsum(
            "qhd,khd->hqk", query_rows, key_tile, preferred_element_type=jnp.float32
        )
        allowed = pos_tile[None, :] <= query_pos[:, None]
        return (jnp.where(allowed[None], raw_scores * score_scale, -1e30), allowed)

    key_tiles = key_all.reshape(block_count, key_block, HEADS, head_dim)
    value_tiles = value_all.reshape(block_count, key_block, HEADS, head_dim)

    def stat_step(carried, tile_set):
        top_prev, total_prev = carried
        scores, allowed = scores_of(tile_set[0], tile_set[1])
        top_new = jnp.maximum(top_prev, jnp.max(scores, axis=-1))
        total_new = total_prev * jnp.exp(top_prev - top_new) + jnp.sum(
            jnp.exp(scores - top_new[..., None]), axis=-1
        )
        return ((top_new, total_new), None)

    start_stats = (
        jnp.full((HEADS, row_count), -1e30, jnp.float32),
        jnp.zeros((HEADS, row_count), jnp.float32),
    )
    (top_all, total_all), _ = lax.scan(stat_step, start_stats, (key_tiles, pos_blocks))
    log_total = top_all + jnp.log(total_all)

    def out_step(summed, tile_set):
        scores, allowed = scores_of(tile_set[0], tile_set[2])
        soft_w = jnp.exp(scores - log_total[..., None]).astype(jnp.bfloat16)
        return (
            summed
            + jnp.einsum("hqk,khd->qhd", soft_w, tile_set[1], preferred_element_type=jnp.float32),
            None,
        )

    heads_f, _ = lax.scan(
        out_step,
        jnp.zeros((row_count, HEADS, head_dim), jnp.float32),
        (key_tiles, value_tiles, pos_blocks),
    )
    heads_low = heads_f.reshape(row_count, model_width).astype(jnp.bfloat16)
    middle = (
        inputs
        + jnp.dot(heads_low, proj_full, preferred_element_type=jnp.float32)
        + proj_b.astype(jnp.float32)
    )
    fsdp_count = lax.axis_size("fsdp")
    width_share = model_width // fsdp_count
    small_stack = jnp.stack([ln2_gain, ln2_bias, out_bias], axis=1)
    small_tiled = jnp.tile(small_stack, (1, fsdp_count))
    fc_cols, small_full = (
        lax.all_to_all(fc_weight, "fsdp", split_axis=1, concat_axis=0, tiled=True),
        lax.all_to_all(small_tiled, "fsdp", split_axis=1, concat_axis=0, tiled=True),
    )
    gain_two_f = small_full[:, 0].astype(jnp.float32)
    shift_two_f = small_full[:, 1].astype(jnp.float32)
    out_b_f = small_full[:, 2].astype(jnp.float32)
    normed_two = layer_norm(middle, gain_two_f, shift_two_f).astype(jnp.bfloat16)
    group_normed, group_upstream = (
        lax.all_gather(normed_two, "fsdp", axis=0, tiled=True),
        lax.all_gather(cotangent, "fsdp", axis=0, tiled=True),
    )
    hidden_pre = jnp.dot(
        group_normed, fc_cols, preferred_element_type=jnp.float32
    ) + fc_bias.astype(jnp.float32)
    hidden = gelu_tanh(hidden_pre).astype(jnp.bfloat16)
    rows = hidden
    summed_out = lax.psum_scatter(
        jnp.dot(rows, out_weight, preferred_element_type=jnp.float32).astype(jnp.bfloat16),
        "fsdp",
        scatter_dimension=0,
        tiled=True,
    ).astype(jnp.float32)
    output = middle + summed_out + out_b_f
    out_rows = output.astype(jnp.bfloat16)
    owned_ow = jnp.einsum("tf,td->fd", hidden, group_upstream, preferred_element_type=jnp.float32)
    full_out_b = jnp.sum(group_upstream.astype(jnp.float32), axis=0)
    owned_ob = lax.dynamic_slice_in_dim(
        full_out_b, lax.axis_index("fsdp") * width_share, width_share, 0
    )
    grad_hidden = jnp.einsum(
        "td,fd->tf", group_upstream, out_weight, preferred_element_type=jnp.float32
    )
    _, gelu_pull = jax.vjp(gelu_tanh, hidden_pre)
    grad_pre = gelu_pull(grad_hidden)[0].astype(jnp.bfloat16)
    grad_fc_cols = jnp.einsum(
        "tc,tf->cf", group_normed, grad_pre, preferred_element_type=jnp.float32
    )
    owned_fcb = jnp.sum(grad_pre.astype(jnp.float32), axis=0)
    rows = grad_pre
    grad_normed_two = lax.psum_scatter(
        jnp.einsum("tf,cf->tc", rows, fc_cols, preferred_element_type=jnp.float32).astype(
            jnp.bfloat16
        ),
        "fsdp",
        scatter_dimension=0,
        tiled=True,
    ).astype(jnp.float32)
    _, norm_pull_two = jax.vjp(layer_norm, middle, gain_two_f, shift_two_f)
    grad_mid_norm, grad_gain_two, grad_shift_two = norm_pull_two(grad_normed_two)
    grad_middle = cotangent.astype(jnp.float32) + grad_mid_norm
    norm_pair = jnp.stack([grad_gain_two, grad_shift_two], axis=1)
    owned_fcw, norm_parts = (
        lax.all_to_all(
            grad_fc_cols.astype(jnp.bfloat16), "fsdp", split_axis=0, concat_axis=1, tiled=True
        ).astype(grad_fc_cols.dtype),
        lax.all_to_all(
            norm_pair.astype(jnp.bfloat16), "fsdp", split_axis=0, concat_axis=1, tiled=True
        ).astype(norm_pair.dtype),
    )
    norm_sums = jnp.sum(norm_parts.reshape(width_share, fsdp_count, 2), axis=1)
    owned_g2 = norm_sums[:, 0]
    owned_b2 = norm_sums[:, 1]
    total_g2, total_b2, total_fcw, total_fcb, total_ow, total_ob = (
        lax.psum(owned_g2.astype(jnp.bfloat16), "ctx").astype(jnp.float32),
        lax.psum(owned_b2.astype(jnp.bfloat16), "ctx").astype(jnp.float32),
        lax.psum(owned_fcw.astype(jnp.bfloat16), "ctx").astype(jnp.float32),
        lax.psum(owned_fcb.astype(jnp.bfloat16), "ctx").astype(jnp.float32),
        lax.psum(owned_ow.astype(jnp.bfloat16), "ctx").astype(jnp.float32),
        lax.psum(owned_ob.astype(jnp.bfloat16), "ctx").astype(jnp.float32),
    )
    grad_branch = grad_middle.astype(jnp.bfloat16)
    grad_proj_w = jnp.einsum(
        "tc,td->cd", heads_low, grad_branch, preferred_element_type=jnp.float32
    )
    grad_proj_b = jnp.sum(grad_branch.astype(jnp.float32), axis=0)
    grad_heads = jnp.einsum(
        "td,cd->tc", grad_branch, proj_full, preferred_element_type=jnp.float32
    ).astype(jnp.bfloat16)
    grad_heads_split = grad_heads.reshape(row_count, HEADS, head_dim)
    delta_rows = jnp.sum(grad_heads_split.astype(jnp.float32) * heads_f, axis=-1).T

    def grad_step(grad_query, tile_set):
        key_tile, value_tile, pos_tile = tile_set
        scores, allowed = scores_of(key_tile, pos_tile)
        soft_w = jnp.exp(scores - log_total[..., None])
        grad_soft = jnp.einsum(
            "qhd,khd->hqk", grad_heads_split, value_tile, preferred_element_type=jnp.float32
        )
        grad_raw = jnp.where(
            allowed[None], soft_w * (grad_soft - delta_rows[..., None]) * score_scale, 0.0
        ).astype(jnp.bfloat16)
        grad_query = grad_query + jnp.einsum(
            "hqk,khd->qhd", grad_raw, key_tile, preferred_element_type=jnp.float32
        )
        grad_key = jnp.einsum(
            "hqk,qhd->khd", grad_raw, query_rows, preferred_element_type=jnp.float32
        )
        grad_value = jnp.einsum(
            "hqk,qhd->khd",
            soft_w.astype(jnp.bfloat16),
            grad_heads_split,
            preferred_element_type=jnp.float32,
        )
        return (grad_query, (grad_key, grad_value))

    grad_query, (key_grads, value_grads) = lax.scan(
        grad_step,
        jnp.zeros((row_count, HEADS, head_dim), jnp.float32),
        (key_tiles, value_tiles, pos_blocks),
    )
    key_terms = key_grads.reshape(seq_len, model_width)
    value_terms = value_grads.reshape(seq_len, model_width)
    key_mine, value_mine = (
        lax.psum_scatter(
            key_terms.astype(jnp.bfloat16), "ctx", scatter_dimension=0, tiled=True
        ).astype(jnp.float32),
        lax.psum_scatter(
            value_terms.astype(jnp.bfloat16), "ctx", scatter_dimension=0, tiled=True
        ).astype(jnp.float32),
    )
    grad_joined = jnp.concatenate(
        [grad_query.reshape(row_count, model_width), key_mine, value_mine], axis=1
    ).astype(jnp.bfloat16)
    grad_q_bias = jnp.sum(grad_joined[:, :model_width].astype(jnp.float32), axis=0)
    grad_v_bias = jnp.sum(grad_joined[:, 2 * model_width :].astype(jnp.float32), axis=0)
    grad_qkv_w = jnp.einsum(
        "tc,tk->ck", normed_one, grad_joined, preferred_element_type=jnp.float32
    )
    grad_normed_one = jnp.einsum(
        "tk,ck->tc", grad_joined, qkv_full, preferred_element_type=jnp.float32
    )
    _, norm_pull_one = jax.vjp(layer_norm, inputs, gain_one_f, shift_one_f)
    grad_in_norm, grad_gain_one, grad_shift_one = norm_pull_one(grad_normed_one)
    grad_inputs = (grad_middle + grad_in_norm).astype(jnp.bfloat16)
    owned_g1, owned_b1, owned_qkv, owned_qb, owned_vb, owned_pw, owned_pb = (
        lax.psum_scatter(
            grad_gain_one.astype(jnp.bfloat16), "fsdp", scatter_dimension=0, tiled=True
        ).astype(jnp.float32),
        lax.psum_scatter(
            grad_shift_one.astype(jnp.bfloat16), "fsdp", scatter_dimension=0, tiled=True
        ).astype(jnp.float32),
        lax.psum_scatter(
            grad_qkv_w.astype(jnp.bfloat16), "fsdp", scatter_dimension=0, tiled=True
        ).astype(jnp.float32),
        lax.psum_scatter(
            grad_q_bias.astype(jnp.bfloat16), "fsdp", scatter_dimension=0, tiled=True
        ).astype(jnp.float32),
        lax.psum_scatter(
            grad_v_bias.astype(jnp.bfloat16), "fsdp", scatter_dimension=0, tiled=True
        ).astype(jnp.float32),
        lax.psum_scatter(
            grad_proj_w.astype(jnp.bfloat16), "fsdp", scatter_dimension=0, tiled=True
        ).astype(jnp.float32),
        lax.psum_scatter(
            grad_proj_b.astype(jnp.bfloat16), "fsdp", scatter_dimension=0, tiled=True
        ).astype(jnp.float32),
    )
    total_g1, total_b1, total_qkv, total_qb, total_vb, total_pw, total_pb = (
        lax.psum(owned_g1.astype(jnp.bfloat16), "ctx").astype(jnp.float32),
        lax.psum(owned_b1.astype(jnp.bfloat16), "ctx").astype(jnp.float32),
        lax.psum(owned_qkv.astype(jnp.bfloat16), "ctx").astype(jnp.float32),
        lax.psum(owned_qb.astype(jnp.bfloat16), "ctx").astype(jnp.float32),
        lax.psum(owned_vb.astype(jnp.bfloat16), "ctx").astype(jnp.float32),
        lax.psum(owned_pw.astype(jnp.bfloat16), "ctx").astype(jnp.float32),
        lax.psum(owned_pb.astype(jnp.bfloat16), "ctx").astype(jnp.float32),
    )
    return (
        out_rows,
        grad_inputs,
        total_g1,
        total_b1,
        total_qkv,
        total_qb,
        total_vb,
        total_pw,
        total_pb,
        total_g2,
        total_b2,
        total_fcw,
        total_fcb,
        total_ow,
        total_ob,
    )


def solution(mesh):
    placed = (
        P(("fsdp", "ctx"), None),
        P(),
        P("fsdp"),
        P("fsdp"),
        P("fsdp", None),
        P("fsdp"),
        P("fsdp"),
        P("fsdp", None),
        P("fsdp"),
        P("fsdp"),
        P("fsdp"),
        P("fsdp", None),
        P("fsdp"),
        P("fsdp", None),
        P("fsdp"),
        P(("fsdp", "ctx"), None),
    )
    return jax.shard_map(
        body,
        mesh=mesh,
        in_specs=placed,
        out_specs=(
            P(("fsdp", "ctx"), None),
            P(("fsdp", "ctx"), None),
            P("fsdp"),
            P("fsdp"),
            P("fsdp", None),
            P("fsdp"),
            P("fsdp"),
            P("fsdp", None),
            P("fsdp"),
            P("fsdp"),
            P("fsdp"),
            P("fsdp", None),
            P("fsdp"),
            P("fsdp", None),
            P("fsdp"),
        ),
        check_vma=False,
    )
```

profile of v0, /device:TPU:0, one launch (start us, length us, event | category | flops | bytes accessed | tf_op | source)
XLA Modules:
  0.0 1569.6 jit_solution(5104515425968146760)
XLA Ops:
  10.6 21.1 %all-reduce.13 = (bf16[1600]{0:T(1024)(128)(2,1)S(1)}, bf16[1600]{0:T(1024)(128)(2,1)S(1)}, bf16[1600]{0:T(1024)(128)(2,1)S(1)}, bf16[1600]{0:T(1024)(128)(2,1)S(1)}, bf16[1600]{0:T(1024)(128)(2,1)S(1)}) all-reduce(bf16[1600]{0:T(1024)(128)(2,1)S(1)} %dynamic-update-slice.2, ...), channel_id=1, replica_groups=mesh['ctx'=8,'fsdp'=4] {'fsdp'}, use_global_device_ids=true, to_apply=%add.2 | all-reduce | flops 8000 | bytes 32000
  32.8 246.5 %all-gather.7.cloned.1.call-done = bf16[1600,4800]{1,0:T(8,128)(2,1)} async-done(((bf16[400,4800]{1,0:T(8,128)(2,1)}), bf16[1600,4800]{1,0:T(8,128)(2,1)}) %all-gather.7.cloned.1.call-update) | async-done | bytes 15360016 | tf_op jit(solution)/shard_map/all_gather | solution.py:55
  279.4 12.1 fusion.80
  294.7 3.3 all-to-all-start
  299.0 11.7 all_to_all.51
  310.7 5.9 copy.78
  316.8 5.1 all-to-all-start.1
  324.4 8.5 reshape.304
  335.8 19.6 %while.39 = (s32[]{:T(128)}, f32[25,128]{1,0:T(8,128)S(1)}, f32[25,128]{1,0:T(8,128)S(1)}, s32[2,512]{1,0:T(2,128)S(1)}, bf16[2,512,25,64]{1,3,2,0:T(8,128)(2,1)...) while((s32[]{:T(128)}, f32[25,128]{1,0:T(8,128)S(1)}, ...), condition=%wide.region_5.6_spmd.clone, body=%wide.region_2.5_spmd.clone.sunk | while | flops 221265664 | bytes 15526528 | solution.py:98
  336.1 5.2 fusion.175
  341.3 4.2 exponential_reduce_fusion.2
  345.9 5.2 fusion.175
  351.1 4.2 exponential_reduce_fusion.2
  355.3 4.9 all-gather.9.cloned.1.call-done
  360.2 8.5 reshape.303
  368.7 4.8 copy.75
  373.5 21.0 %while.40 = (s32[]{:T(128)}, f32[128,25,64]{0,2,1:T(8,128)}, bf16[2,512,25,64]{1,3,2,0:T(8,128)(2,1)}, s32[2,512]{1,0:T(2,128)S(1)}, bf16[2,512,25,64]{1,3,2,0:T...) while((s32[]{:T(128)}, f32[128,25,64]{0,2,1:T(8,128)}, ...), condition=%wide.region_7.8_spmd.clone, body=%wide.region_6.7_spmd.clone.sunk | while | flops 426459264 | bytes 5482114 | solution.py:110
  373.8 4.7 fusion.181
  378.8 5.0 fusion.181
  396.5 129.3 %all-gather.13.cloned.1.call-done = bf16[1600,1600]{1,0:T(8,128)(2,1)} async-done(((bf16[400,1600]{1,0:T(8,128)(2,1)}), bf16[1600,1600]{1,0:T(8,128)(2,1)}) %all-gather.13.cloned.1.call-update) | async-done | bytes 5120016 | tf_op jit(solution)/shard_map/all_gather | solution.py:58
  525.8 5.0 fusion.125
  533.0 31.9 %all-gather.17.cloned.1.call-done = bf16[512,1600]{0,1:T(8,128)(2,1)} async-done(((bf16[128,1600]{0,1:T(8,128)(2,1)}), bf16[512,1600]{0,1:T(8,128)(2,1)}) %all-gather.17.cloned.1.call-update) | async-done | bytes 1638416 | tf_op jit(solution)/shard_map/all_gather | solution.py:135
  564.9 7.9 fusion.126
  572.8 31.1 %all-gather.15.cloned.1.call-done = bf16[512,1600]{0,1:T(8,128)(2,1)} async-done(((bf16[128,1600]{0,1:T(8,128)(2,1)}), bf16[512,1600]{0,1:T(8,128)(2,1)}) %all-gather.15.cloned.1.call-update) | async-done | bytes 1638416 | tf_op jit(solution)/shard_map/all_gather | solution.py:134
  603.9 11.7 fusion.118
  616.8 6.7 convolution_convert_fusion.4
  623.5 3.5 copy.91
  627.1 35.8 %reduce-scatter.21.cloned.1.call-done = bf16[128,1600]{1,0:T(8,128)(2,1)} async-done(((bf16[512,1600]{1,0:T(8,128)(2,1)}), bf16[128,1600]{1,0:T(8,128)(2,1)}) %reduce-scatter.21.cloned.1.call-update) | async-done | bytes 409616
  670.4 4.2 convolution_convert_fusion.6
  675.4 49.1 %while.41 = (s32[]{:T(128)}, f32[128,25,64]{0,2,1:T(8,128)}, bf16[2,512,25,64]{1,3,2,0:T(8,128)(2,1)}, bf16[2,512,25,64]{1,3,2,0:T(8,128)(2,1)}, bf16[2,512,25,6...) while((s32[]{:T(128)}, f32[128,25,64]{0,2,1:T(8,128)}, ...), condition=%wide.region_16.17_spmd.clone, body=%wide.region_15.16_spmd.clone.sunk | while | flops 1068712064 | bytes 150980000 | solution.py:231
  675.8 5.2 fusion.192
  681.3 6.4 fusion.193
  687.7 3.3 fusion.194
  695.2 3.1 bitcast_dynamic-update-slice_fusion.5
  700.1 5.1 fusion.192
  705.5 6.4 fusion.193
  712.0 3.5 fusion.194
  719.7 3.1 bitcast_dynamic-update-slice_fusion.5
  724.5 5.3 copy.82
  730.7 3.5 copy.95
  736.2 3.4 copy.81
  740.5 3.5 copy.93
  745.2 3.9 convolution_convert_fusion.3
  750.5 30.1 %reduce-scatter.25.cloned.1.call-done = bf16[128,1600]{1,0:T(8,128)(2,1)} async-done(((bf16[1024,1600]{1,0:T(8,128)(2,1)}), bf16[128,1600]{1,0:T(8,128)(2,1)}) %reduce-scatter.25.cloned.1.call-update) | async-done | bytes 409616
  781.9 50.1 %reduce-scatter.23.cloned.1.call-done = bf16[128,1600]{1,0:T(8,128)(2,1)} async-done(((bf16[1024,1600]{1,0:T(8,128)(2,1)}), bf16[128,1600]{1,0:T(8,128)(2,1)}) %reduce-scatter.23.cloned.1.call-update) | async-done | bytes 409616
  833.4 8.5 convolution_convert_fusion
  843.3 6.3 convolution_convert_fusion.2
  849.6 5.1 all-to-all-start.3
  855.0 8.0 convolution_convert_fusion.5
  863.0 3.7 copy.89
  866.8 8.1 convolution_convert_fusion.1
  874.9 176.1 %all-to-all-done.3 = bf16[4,400,1600]{2,1,0:T(8,128)(2,1)} async-done(((bf16[4,400,1600]{2,1,0:T(8,128)(2,1)}), bf16[4,400,1600]{2,1,0:T(8,128)(2,1)}, u32[]{:S(2)}, u32[]{:S(2)}) %all-to-all-start.3) | async-done | bytes 5120032 | tf_op jit(solution)/shard_map/all_to_all | solution.py:178
  1051.0 6.9 copy.84
  1057.9 9.8 all_to_all.59
  1067.8 228.2 %reduce-scatter.15.cloned.1.call-done = bf16[400,4800]{1,0:T(8,128)(2,1)} async-done(((bf16[1600,4800]{1,0:T(8,128)(2,1)}), bf16[400,4800]{1,0:T(8,128)(2,1)}) %reduce-scatter.15.cloned.1.call-update) | async-done | bytes 3840016 | tf_op jit(solution)/shard_map/reduce_scatter | solution.py:267
  1297.9 3.5 all-to-all-start.2
  1301.9 33.4 %reduce-scatter.19.cloned.1.call-done = bf16[128,1600]{1,0:T(8,128)(2,1)} async-done(((bf16[512,1600]{1,0:T(8,128)(2,1)}), bf16[128,1600]{1,0:T(8,128)(2,1)}) %reduce-scatter.19.cloned.1.call-update) | async-done | bytes 409616
  1336.7 9.3 fusion.117
  1346.6 16.9 %all-reduce.12 = (bf16[1600]{0:T(1024)(128)(2,1)S(1)}, bf16[1600]{0:T(1024)(128)(2,1)S(1)}, bf16[1600]{0:T(1024)(128)(2,1)S(1)}, bf16[1600]{0:T(1024)(128)(2,1)S(1)}, bf16[1600]{0:T(1024)(128)(2,1)S(1)}) all-reduce(bf16[1600]{0:T(1024)(128)(2,1)S(1)} %get-tuple-element.374, ...), channel_id=6, replica_groups=mesh['ctx'=8,'fsdp'=4] {'fsdp'}, use_global_device_ids=true, to_apply=%region_22.23.clone | all-reduce | flops 8000 | bytes 32000
  1363.9 24.1 %all-reduce.10 = (bf16[400]{0:T(512)(128)(2,1)S(1)}, bf16[400]{0:T(512)(128)(2,1)S(1)}, bf16[400]{0:T(512)(128)(2,1)S(1)}, bf16[400]{0:T(512)(128)(2,1)S(1)}, bf...) all-reduce(bf16[400]{0:T(512)(128)(2,1)S(1)} %dynamic-slice.6, ...), channel_id=1, replica_groups=mesh['ctx'=8,'fsdp'=4] {'ctx'}, use_global_device_ids=true, to_apply=%region_23.24 | all-reduce | flops 4800 | bytes 19200 | tf_op jit(solution)/shard_map/psum | solution.py:284
  1395.2 150.3 %all-reduce.16.cloned.1.call-done = (bf16[400,4800]{1,0:T(8,128)(2,1)}, bf16[400,1600]{1,0:T(8,128)(2,1)}, bf16[400,6400]{1,0:T(8,128)(2,1)}, bf16[1600,1600]{1,0:T(8,128)(2,1)}) async-done(((bf16[400,4800]{1,0:T(8,128)(2,1)}, bf16[400,1600]{1,0:T(8,128)(2,1)}, bf16[400,6400]{1,0:T(8,128)(2,1)}, bf16[1600,1600]{1,0:T(8,128)(2,1)}), (bf16[400,4800]{1,0:T(8,128)(2,1)}, bf16[400,1600]{1,0:T(8,128)(2,1)}, ...) | async-done | bytes 15360016 | tf_op jit(solution)/shard_map/psum | solution.py:286
  1545.5 6.0 convert_element_type.266
  1553.2 4.7 convert_element_type.278
  1557.9 4.8 convert_element_type.281
  (291 shorter events, 63.9 us)
Async XLA Ops:
  7.2 2.6 copy-start.46
  7.2 2.9 copy-start.47
  7.2 3.1 copy-start.48
  7.2 24.6 %copy-start.7 = (bf16[128,1600]{0,1:T(8,128)(2,1)S(1)}, bf16[128,1600]{0,1:T(8,128)(2,1)}, u32[]{:S(2)}) copy-start(bf16[128,1600]{0,1:T(8,128)(2,1)} %param.22) | copy-start | bytes 1228804
  7.3 272.1 %all-gather.7.cloned.1.call-start = ((), (), s32[]{:S(2)}) async-start(), calls=%async_computation.10 | async-start | bytes 19456000 | tf_op jit(solution)/shard_map/all_gather | solution.py:55
  8.0 316.4 %all-gather.11.cloned.1.call-start = ((), (), s32[]{:S(2)}) async-start(), calls=%async_computation.12 | async-start | bytes 3686400 | tf_op jit(solution)/shard_map/all_gather | solution.py:71
  31.7 259.8 %copy-start.28 = (f32[1600]{0:T(1024)}, f32[1600]{0:T(1024)S(1)}, u32[]{:S(2)}) copy-start(f32[1600]{0:T(1024)S(1)} %convert_element_type.230) | copy-start | bytes 19204
  31.8 259.7 %copy-start.30 = (f32[1600]{0:T(1024)}, f32[1600]{0:T(1024)S(1)}, u32[]{:S(2)}) copy-start(f32[1600]{0:T(1024)S(1)} %convert_element_type.231) | copy-start | bytes 19204
  32.1 259.4 %copy-start.33 = (f32[128]{0:T(128)}, f32[128]{0:T(128)S(1)}, u32[]{:S(2)}) copy-start(f32[128]{0:T(128)S(1)} %broadcast_multiply_fusion.2) | copy-start | bytes 1540
  32.8 258.7 %copy-start.35 = (f32[128]{0:T(128)}, f32[128]{0:T(128)S(1)}, u32[]{:S(2)}) copy-start(f32[128]{0:T(128)S(1)} %fusion.110) | copy-start | bytes 1540
  291.6 7.0 copy-start.39
  292.7 67.6 %all-gather.9.cloned.1.call-start = ((), (), s32[]{:S(2)}) async-start(), calls=%async_computation.11 | async-start | bytes 3686400 | tf_op jit(solution)/shard_map/all_gather | solution.py:72
  293.4 232.4 %all-gather.13.cloned.1.call-start = ((), (), s32[]{:S(2)}) async-start(), calls=%async_computation.13 | async-start | bytes 6656000 | tf_op jit(solution)/shard_map/all_gather | solution.py:58
  294.7 22.1 %all-to-all-start = ((bf16[400,4,3]{0,2,1:T(4,128)(2,1)}), bf16[400,4,3]{0,2,1:T(4,128)(2,1)S(1)}, u32[]{:S(2)}, u32[]{:S(2)}) async-start(bf16[400,4,3]{0,2,1:T(4,128)(2,1)} %tile.2), calls=%async_computation | async-start | bytes 32768 | tf_op jit(solution)/shard_map/all_to_all | solution.py:127
  297.9 267.0 %all-gather.17.cloned.1.call-start = ((), (), s32[]{:S(2)}) async-start(), calls=%async_computation.15 | async-start | bytes 2048000 | tf_op jit(solution)/shard_map/all_gather | solution.py:135
  316.8 256.0 %all-to-all-start.1 = ((bf16[400,4,1600]{2,0,1:T(8,128)(2,1)}), bf16[400,4,1600]{2,0,1:T(8,128)(2,1)}, u32[]{:S(2)}, u32[]{:S(2)}) async-start(bf16[400,4,1600]{2,0,1:T(8,128)(2,1)} %copy.78), calls=%async_computation.1 | async-start | bytes 10649600 | tf_op jit(solution)/shard_map/all_to_all | solution.py:126
  321.9 282.0 %all-gather.15.cloned.1.call-start = ((), (), s32[]{:S(2)}) async-start(), calls=%async_computation.14 | async-start | bytes 2048000 | tf_op jit(solution)/shard_map/all_gather | solution.py:134
  525.8 7.2 copy-start.37
  532.9 130.0 %reduce-scatter.21.cloned.1.call-start = ((), (), s32[]{:S(2)}) async-start(), calls=%async_computation.19 | async-start | bytes 2129920
  627.1 153.6 %reduce-scatter.25.cloned.1.call-start = ((), (), s32[]{:S(2)}) async-start(), calls=%async_computation.21 | async-start | bytes 3833856
  670.4 4.3 copy-start.24
  670.4 4.3 copy-start.17
  675.8 5.2 copy-start
  687.7 3.4 copy-start.3
  687.7 3.4 copy-start.12
  687.7 4.6 copy-start.15
  691.1 4.2 copy-start.2
  692.3 6.0 copy-start.13
  695.2 4.8 copy-start.1
  700.1 5.2 copy-start
  711.9 3.6 copy-start.3
  711.9 3.6 copy-start.12
  712.0 4.8 copy-start.15
  715.5 4.2 copy-start.2
  716.8 6.0 copy-start.13
  719.7 4.8 copy-start.1
  734.3 97.8 %reduce-scatter.23.cloned.1.call-start = ((), (), s32[]{:S(2)}) async-start(), calls=%async_computation.20 | async-start | bytes 3833856
  744.0 323.8 %reduce-scatter.17.cloned.1.call-start = ((), (), s32[]{:S(2)}) async-start(), calls=%async_computation.17 | async-start | bytes 6656000 | tf_op jit(solution)/shard_map/reduce_scatter | solution.py:276
  749.1 84.2 %copy-start.8 = (bf16[128,1600]{0,1:T(8,128)(2,1)S(1)}, bf16[128,1600]{0,1:T(8,128)(2,1)}, u32[]{:S(2)}) copy-start(bf16[128,1600]{0,1:T(8,128)(2,1)} %param.22) | copy-start | bytes 1228804
  749.1 84.2 %copy-start.29 = (f32[1600]{0:T(1024)S(1)}, f32[1600]{0:T(1024)}, u32[]{:S(2)}) copy-start(f32[1600]{0:T(1024)} %copy-done.28) | copy-start | bytes 19204
  749.1 84.2 %copy-start.31 = (f32[1600]{0:T(1024)S(1)}, f32[1600]{0:T(1024)}, u32[]{:S(2)}) copy-start(f32[1600]{0:T(1024)} %copy-done.30) | copy-start | bytes 19204
  749.1 84.2 %copy-start.34 = (f32[128]{0:T(128)S(1)}, f32[128]{0:T(128)}, u32[]{:S(2)}) copy-start(f32[128]{0:T(128)} %copy-done.33) | copy-start | bytes 1540
  749.1 84.2 %copy-start.36 = (f32[128]{0:T(128)S(1)}, f32[128]{0:T(128)}, u32[]{:S(2)}) copy-start(f32[128]{0:T(128)} %copy-done.35) | copy-start | bytes 1540
  749.1 546.8 %reduce-scatter.15.cloned.1.call-start = ((), (), s32[]{:S(2)}) async-start(), calls=%async_computation.16 | async-start | bytes 19456000 | tf_op jit(solution)/shard_map/reduce_scatter | solution.py:267
  750.5 91.3 %copy-start.21 = (bf16[128,25,64]{0,2,1:T(8,128)(2,1)}, bf16[128,25,64]{0,2,1:T(8,128)(2,1)S(1)}, u32[]{:S(2)}) copy-start(bf16[128,25,64]{0,2,1:T(8,128)(2,1)S(1)} %get-tuple-element.465) | copy-start | bytes 1228804
  781.9 59.9 %copy-start.22 = (bf16[128,1600]{0,1:T(8,128)(2,1)}, bf16[128,1600]{0,1:T(8,128)(2,1)S(1)}, u32[]{:S(2)}) copy-start(bf16[128,1600]{0,1:T(8,128)(2,1)S(1)} %copy.96) | copy-start | bytes 1228804
  833.3 8.5 copy-start.23
  849.6 201.4 %all-to-all-start.3 = ((bf16[4,400,1600]{2,1,0:T(8,128)(2,1)}), bf16[4,400,1600]{2,1,0:T(8,128)(2,1)}, u32[]{:S(2)}, u32[]{:S(2)}) async-start(bf16[4,400,1600]{2,1,0:T(8,128)(2,1)} %bitcast.213), calls=%async_computation.5 | async-start | bytes 10649600 | tf_op jit(solution)/shard_map/all_to_all | solution.py:178
  854.7 480.5 %reduce-scatter.19.cloned.1.call-start = ((), (), s32[]{:S(2)}) async-start(), calls=%async_computation.18 | async-start | bytes 2129920
  863.0 3.7 copy-start.20
  866.7 678.8 %all-reduce.16.cloned.1.call-start = ((), (), s32[]{:S(2)}) async-start(), calls=%async_computation.22 | async-start | bytes 31334400 | tf_op jit(solution)/shard_map/psum | solution.py:286
  1296.0 40.5 %copy-start.19 = (bf16[128,1600]{1,0:T(8,128)(2,1)S(1)}, bf16[128,1600]{1,0:T(8,128)(2,1)}, u32[]{:S(2)}) copy-start(bf16[128,1600]{1,0:T(8,128)(2,1)} %reduce-scatter.25.cloned.1.call-done) | copy-start | bytes 1228804
  1297.9 38.6 %all-to-all-start.2 = ((bf16[4,400,2]{1,2,0:T(2,128)(2,1)}), bf16[4,400,2]{1,2,0:T(2,128)(2,1)S(1)}, u32[]{:S(2)}, u32[]{:S(2)}) async-start(bf16[4,400,2]{1,2,0:T(2,128)(2,1)} %copy.83), calls=%async_computation.4 | async-start | bytes 16384 | tf_op jit(solution)/shard_map/all_to_all | solution.py:181
  1336.6 9.4 copy-start.50
  1336.6 27.3 %copy-start.38 = (bf16[1600]{0:T(1024)(128)(2,1)S(1)}, bf16[1600]{0:T(1024)(128)(2,1)}, u32[]{:S(2)}) copy-start(bf16[1600]{0:T(1024)(128)(2,1)} %get-tuple-element.460) | copy-start | bytes 9604
  1336.6 56.7 %copy-start.5 = (f32[128,1600]{0,1:T(8,128)S(1)}, f32[128,1600]{0,1:T(8,128)}, u32[]{:S(2)}) copy-start(f32[128,1600]{0,1:T(8,128)} %copy-done.4) | copy-start | bytes 2457604
  1336.6 56.7 %copy-start.9 = (bf16[128,1600]{0,1:T(8,128)(2,1)S(1)}, bf16[128,1600]{0,1:T(8,128)(2,1)}, u32[]{:S(2)}) copy-start(bf16[128,1600]{0,1:T(8,128)(2,1)} %copy.92) | copy-start | bytes 1228804
  1336.7 56.7 %copy-start.11 = (bf16[128,1600]{0,1:T(8,128)(2,1)S(1)}, bf16[128,1600]{0,1:T(8,128)(2,1)}, u32[]{:S(2)}) copy-start(bf16[128,1600]{0,1:T(8,128)(2,1)} %param.37) | copy-start | bytes 1228804
  1336.7 56.6 %copy-start.32 = (f32[1600]{0:T(1024)S(1)}, f32[1600]{0:T(1024)}, u32[]{:S(2)}) copy-start(f32[1600]{0:T(1024)} %get-tuple-element.378) | copy-start | bytes 19204
  1545.5 7.6 slice-start.2
  1545.5 6.0 copy-start.26
  1545.5 7.6 slice-start.3
  1551.5 6.4 slice-start
  1553.2 4.7 slice-start.1
  (18 other events, 27.3 us)
Sparse Core Ops, SparseCore 0:
  9.6 269.6 all-gather.6
  292.8 31.6 all-gather.10
  326.9 33.2 all-gather.8
  361.7 164.0 all-gather.12
  527.2 37.6 all-gather.16
  566.9 36.9 all-gather.14
  627.2 35.6 reduce-scatter.20
  734.4 46.2 reduce-scatter.24
  784.7 47.3 reduce-scatter.22
  834.8 164.3 reduce-scatter.16
  1001.5 294.3 reduce-scatter.14
  1298.7 36.4 reduce-scatter.18
  1339.8 205.6 all-reduce.15
where the time goes:
time: 1580 us; the launch traced here: 1570 us
  waiting for transfers between devices  1150 us (73%)
  matrix products  151 us (10%)
  local copies, waits for them, and re-layouts  113 us (7%)
  blocking collectives  62.2 us (4%)
  other arithmetic  45.8 us (3%)
  starting transfers between devices  18.1 us (1%)
  between operations  16.5 us (1%)
    all_gather x1, waiting for transfers between devices, body(): lax.all_gather(qkv_weight, 'fsdp', axis=0, tiled=True)  247 us
    reduce_scatter x1, waiting for transfers between devices, body(): lax.psum_scatter(grad_qkv_w.astype(jnp.bfloat16), 'fsdp', scatter_dimensi...  228 us
    all_to_all x1, waiting for transfers between devices, body(): lax.all_to_all(grad_fc_cols.astype(jnp.bfloat16), 'fsdp', split_axis=0, c...  176 us
    unnamed x17, waiting for transfers between devices  152 us
    psum x1, waiting for transfers between devices, body(): lax.psum(owned_qkv.astype(jnp.bfloat16), 'ctx').astype(jnp.float32)  150 us
    all_gather x1, waiting for transfers between devices, body(): lax.all_gather(proj_weight, 'fsdp', axis=0, tiled=True)  129 us
    unnamed x127, local copies, waits for them, and re-layouts  40.2 us
    unnamed x2, blocking collectives  38 us
  transfers between devices with their start and end apart: 17, of which 13 were waited for; matrix products, arithmetic and copies ran while one was open for 10% of the time, Pallas kernels for 0%

commit v1 on v0

--- a/solution.py
+++ b/solution.py
@@ -5,6 +5,18 @@
 from jax.sharding import PartitionSpec as P
 
 HEADS = 25
+
+
+def collect(shard, axis, dim):
+    ways, here = (lax.axis_size(axis), lax.axis_index(axis))
+    grown, reach = (shard, 1)
+    while reach < ways:
+        theirs = lax.ppermute(grown, axis, [(d, d ^ reach) for d in range(ways)])
+        mine_first = jnp.concatenate([grown, theirs], axis=dim)
+        theirs_first = jnp.concatenate([theirs, grown], axis=dim)
+        grown = jnp.where(here & reach == 0, mine_first, theirs_first)
+        reach = 2 * reach
+    return grown
 
 
 def layer_norm(values, gain_vec, shift_vec):
@@ -55,7 +67,7 @@
         lax.all_gather(qkv_weight, "fsdp", axis=0, tiled=True),
         lax.all_gather(query_bias, "fsdp", axis=0, tiled=True),
         lax.all_gather(value_bias, "fsdp", axis=0, tiled=True),
-        lax.all_gather(proj_weight, "fsdp", axis=0, tiled=True),
+        collect(proj_weight, "fsdp", 0),
         lax.all_gather(proj_bias, "fsdp", axis=0, tiled=True),
     )
     inputs = tokens.astype(jnp.float32)

time: 1580 us -> 1610 us (1.019)
  waiting for transfers between devices: 1150 us -> 1190 us
    ppermute x0 -> x2, waiting for transfers between devices: none -> 195 us  [collect(): theirs = lax.ppermute(grown, axis, [(d, d ^ reach) for d in range(ways)])]
    all_gather x1 -> x0, waiting for transfers between devices: 129 us -> none  [body(): lax.all_gather(proj_weight, 'fsdp', axis=0, tiled=True)]
    all_gather x1, waiting for transfers between devices: 31.9 us -> 0.02 us  [body(): lax.all_gather(cotangent, 'fsdp', axis=0, tiled=True)]
    unnamed x127 -> x131, local copies, waits for them, and re-layouts: 40.2 us -> 39.7 us
    unnamed x17 -> x16, waiting for transfers between devices: 152 us -> 152 us
  transfers between devices with their start and end apart: 17 -> 18, of which waited for: 13 -> 11; matrix products, arithmetic and copies ran while one was open for 10% -> 10% of each run, Pallas kernels for 0% -> 0%
where the time goes in v1:
time: 1610 us; the launch traced here: 1600 us
  waiting for transfers between devices  1190 us (74%)
  matrix products  155 us (10%)
  local copies, waits for them, and re-layouts  113 us (7%)
  blocking collectives  62.3 us (4%)
  other arithmetic  47.6 us (3%)
  starting transfers between devices  20.4 us (1%)
  between operations  16.6 us (1%)
    all_gather x1, waiting for transfers between devices, body(): lax.all_gather(qkv_weight, 'fsdp', axis=0, tiled=True)  247 us
    reduce_scatter x1, waiting for transfers between devices, body(): lax.psum_scatter(grad_qkv_w.astype(jnp.bfloat16), 'fsdp', scatter_dimensi...  228 us
    ppermute x2, waiting for transfers between devices, collect(): theirs = lax.ppermute(grown, axis, [(d, d ^ reach) for d in range(ways)])  195 us
    all_to_all x1, waiting for transfers between devices, body(): lax.all_to_all(grad_fc_cols.astype(jnp.bfloat16), 'fsdp', split_axis=0, c...  176 us
    unnamed x16, waiting for transfers between devices  152 us
    psum x1, waiting for transfers between devices, body(): lax.psum(owned_qkv.astype(jnp.bfloat16), 'ctx').astype(jnp.float32)  150 us
    unnamed x131, local copies, waits for them, and re-layouts  39.7 us
    unnamed x2, blocking collectives  38 us
  transfers between devices with their start and end apart: 18, of which 11 were waited for; matrix products, arithmetic and copies ran while one was open for 10% of the time, Pallas kernels for 0%

profile of v1, /device:TPU:0, one launch (start us, length us, event | category | flops | bytes accessed | tf_op | source)
XLA Modules:
  0.0 1602.5 jit_solution(6057637392929540786)
XLA Ops:
  10.6 21.1 %all-reduce.13 = (bf16[1600]{0:T(1024)(128)(2,1)S(1)}, bf16[1600]{0:T(1024)(128)(2,1)S(1)}, bf16[1600]{0:T(1024)(128)(2,1)S(1)}, bf16[1600]{0:T(1024)(128)(2,1)S(1)}, bf16[1600]{0:T(1024)(128)(2,1)S(1)}) all-reduce(bf16[1600]{0:T(1024)(128)(2,1)S(1)} %dynamic-update-slice.2, ...), channel_id=1, replica_groups=mesh['ctx'=8,'fsdp'=4] {'fsdp'}, use_global_device_ids=true, to_apply=%add.2 | all-reduce | flops 8000 | bytes 32000
  32.8 246.5 %all-gather.6.cloned.1.call-done = bf16[1600,4800]{1,0:T(8,128)(2,1)} async-done(((bf16[400,4800]{1,0:T(8,128)(2,1)}), bf16[1600,4800]{1,0:T(8,128)(2,1)}) %all-gather.6.cloned.1.call-update) | async-done | bytes 15360016 | tf_op jit(solution)/shard_map/all_gather | solution.py:67
  279.4 12.1 fusion.80
  294.2 3.3 all-to-all-start
  298.5 11.7 all_to_all.51
  310.2 6.0 copy.78
  316.4 8.4 all-to-all-done
  324.9 5.1 all-to-all-start.1
  336.1 8.5 reshape.304
  347.2 19.6 %while.39 = (s32[]{:T(128)}, f32[25,128]{1,0:T(8,128)S(1)}, f32[25,128]{1,0:T(8,128)S(1)}, s32[2,512]{1,0:T(2,128)S(1)}, bf16[2,512,25,64]{1,3,2,0:T(8,128)(2,1)...) while((s32[]{:T(128)}, f32[25,128]{1,0:T(8,128)S(1)}, ...), condition=%wide.region_5.6_spmd.clone, body=%wide.region_2.5_spmd.clone.sunk | while | flops 221265664 | bytes 15526528 | solution.py:110
  347.5 5.2 fusion.175
  352.8 4.3 exponential_reduce_fusion.2
  357.4 5.2 fusion.175
  362.6 4.2 exponential_reduce_fusion.2
  366.9 8.5 reshape.303
  375.4 4.4 copy.75
  379.8 10.8 while.40
  380.1 4.7 fusion.181
  385.2 5.0 fusion.181
  391.8 195.5 %collective-permute-done.1 = bf16[800,1600]{1,0:T(8,128)(2,1)} collective-permute-done((bf16[800,1600]{1,0:T(8,128)(2,1)}, bf16[800,1600]{1,0:T(8,128)(2,1)}, u32[]{:S(2)}, u32[]{:S(2)}) %collective-permute-start.1) | collective-permute-done | bytes 2560032 | tf_op jit(solution)/shard_map/ppermute | solution.py:14
  587.3 7.1 fusion.127
  596.7 7.9 fusion.128
  604.6 30.0 %all-gather.12.cloned.1.call-done = bf16[512,1600]{0,1:T(8,128)(2,1)} async-done(((bf16[128,1600]{0,1:T(8,128)(2,1)}), bf16[512,1600]{0,1:T(8,128)(2,1)}) %all-gather.12.cloned.1.call-update) | async-done | bytes 1638416 | tf_op jit(solution)/shard_map/all_gather | solution.py:146
  634.6 11.7 fusion.120
  647.4 6.9 convolution_convert_fusion.4
  654.3 3.5 copy.91
  657.9 35.8 %reduce-scatter.21.cloned.1.call-done = bf16[128,1600]{1,0:T(8,128)(2,1)} async-done(((bf16[512,1600]{1,0:T(8,128)(2,1)}), bf16[128,1600]{1,0:T(8,128)(2,1)}) %reduce-scatter.21.cloned.1.call-update) | async-done | bytes 409616
  701.1 6.4 convolution_convert_fusion.6
  708.3 48.8 %while.41 = (s32[]{:T(128)}, f32[128,25,64]{0,2,1:T(8,128)}, bf16[2,512,25,64]{1,3,2,0:T(8,128)(2,1)}, bf16[2,512,25,64]{1,3,2,0:T(8,128)(2,1)}, bf16[2,512,25,6...) while((s32[]{:T(128)}, f32[128,25,64]{0,2,1:T(8,128)}, ...), condition=%wide.region_16.17_spmd.clone, body=%wide.region_15.16_spmd.clone.sunk | while | flops 1068712064 | bytes 150980000 | solution.py:243
  708.3 5.1 fusion.192
  713.8 6.4 fusion.193
  720.2 3.3 fusion.194
  727.6 3.1 bitcast_dynamic-update-slice_fusion.5
  732.5 5.1 fusion.192
  737.9 6.4 fusion.193
  744.4 3.5 fusion.194
  749.1 2.9 copy-done.2
  752.0 3.1 bitcast_dynamic-update-slice_fusion.5
  757.1 5.3 copy.82
  763.3 3.5 copy.95
  768.7 3.4 copy.81
  773.0 3.5 copy.93
  777.7 3.9 convolution_convert_fusion.3
  783.1 30.1 %reduce-scatter.25.cloned.1.call-done = bf16[128,1600]{1,0:T(8,128)(2,1)} async-done(((bf16[1024,1600]{1,0:T(8,128)(2,1)}), bf16[128,1600]{1,0:T(8,128)(2,1)}) %reduce-scatter.25.cloned.1.call-update) | async-done | bytes 409616
  814.5 50.1 %reduce-scatter.23.cloned.1.call-done = bf16[128,1600]{1,0:T(8,128)(2,1)} async-done(((bf16[1024,1600]{1,0:T(8,128)(2,1)}), bf16[128,1600]{1,0:T(8,128)(2,1)}) %reduce-scatter.23.cloned.1.call-update) | async-done | bytes 409616
  865.9 8.9 convolution_convert_fusion
  876.3 6.3 convolution_convert_fusion.2
  882.6 5.1 all-to-all-start.3
  887.7 8.0 convolution_convert_fusion.5
  895.8 3.7 copy.89
  899.7 8.1 convolution_convert_fusion.1
  907.8 176.2 %all-to-all-done.3 = bf16[4,400,1600]{2,1,0:T(8,128)(2,1)} async-done(((bf16[4,400,1600]{2,1,0:T(8,128)(2,1)}), bf16[4,400,1600]{2,1,0:T(8,128)(2,1)}, u32[]{:S(2)}, u32[]{:S(2)}) %all-to-all-start.3) | async-done | bytes 5120032 | tf_op jit(solution)/shard_map/all_to_all | solution.py:190
  1084.0 6.9 copy.84
  1091.0 9.8 all_to_all.59
  1100.8 227.9 %reduce-scatter.15.cloned.1.call-done = bf16[400,4800]{1,0:T(8,128)(2,1)} async-done(((bf16[1600,4800]{1,0:T(8,128)(2,1)}), bf16[400,4800]{1,0:T(8,128)(2,1)}) %reduce-scatter.15.cloned.1.call-update) | async-done | bytes 3840016 | tf_op jit(solution)/shard_map/reduce_scatter | solution.py:279
  1330.6 3.2 all-to-all-start.2
  1334.3 33.8 %reduce-scatter.19.cloned.1.call-done = bf16[128,1600]{1,0:T(8,128)(2,1)} async-done(((bf16[512,1600]{1,0:T(8,128)(2,1)}), bf16[128,1600]{1,0:T(8,128)(2,1)}) %reduce-scatter.19.cloned.1.call-update) | async-done | bytes 409616
  1369.6 9.3 fusion.119
  1379.5 16.9 %all-reduce.12 = (bf16[1600]{0:T(1024)(128)(2,1)S(1)}, bf16[1600]{0:T(1024)(128)(2,1)S(1)}, bf16[1600]{0:T(1024)(128)(2,1)S(1)}, bf16[1600]{0:T(1024)(128)(2,1)S(1)}, bf16[1600]{0:T(1024)(128)(2,1)S(1)}) all-reduce(bf16[1600]{0:T(1024)(128)(2,1)S(1)} %get-tuple-element.374, ...), channel_id=6, replica_groups=mesh['ctx'=8,'fsdp'=4] {'fsdp'}, use_global_device_ids=true, to_apply=%region_22.23.clone | all-reduce | flops 8000 | bytes 32000
  1396.8 24.2 %all-reduce.10 = (bf16[400]{0:T(512)(128)(2,1)S(1)}, bf16[400]{0:T(512)(128)(2,1)S(1)}, bf16[400]{0:T(512)(128)(2,1)S(1)}, bf16[400]{0:T(512)(128)(2,1)S(1)}, bf...) all-reduce(bf16[400]{0:T(512)(128)(2,1)S(1)} %dynamic-slice.6, ...), channel_id=1, replica_groups=mesh['ctx'=8,'fsdp'=4] {'ctx'}, use_global_device_ids=true, to_apply=%region_23.24 | all-reduce | flops 4800 | bytes 19200 | tf_op jit(solution)/shard_map/psum | solution.py:296
  1428.2 150.0 %all-reduce.16.cloned.1.call-done = (bf16[400,4800]{1,0:T(8,128)(2,1)}, bf16[400,1600]{1,0:T(8,128)(2,1)}, bf16[400,6400]{1,0:T(8,128)(2,1)}, bf16[1600,1600]{1,0:T(8,128)(2,1)}) async-done(((bf16[400,4800]{1,0:T(8,128)(2,1)}, bf16[400,1600]{1,0:T(8,128)(2,1)}, bf16[400,6400]{1,0:T(8,128)(2,1)}, bf16[1600,1600]{1,0:T(8,128)(2,1)}), (bf16[400,4800]{1,0:T(8,128)(2,1)}, bf16[400,1600]{1,0:T(8,128)(2,1)}, ...) | async-done | bytes 15360016 | tf_op jit(solution)/shard_map/psum | solution.py:298
  1578.3 6.0 convert_element_type.266
  1585.9 4.7 convert_element_type.278
  1590.6 4.8 convert_element_type.281
  (297 shorter events, 63.1 us)
Async XLA Ops:
  7.2 3.1 copy-start.50
  7.2 24.6 %copy-start.7 = (bf16[128,1600]{0,1:T(8,128)(2,1)S(1)}, bf16[128,1600]{0,1:T(8,128)(2,1)}, u32[]{:S(2)}) copy-start(bf16[128,1600]{0,1:T(8,128)(2,1)} %param.22) | copy-start | bytes 1228804
  7.3 272.1 %all-gather.6.cloned.1.call-start = ((), (), s32[]{:S(2)}) async-start(), calls=%async_computation.10 | async-start | bytes 19456000 | tf_op jit(solution)/shard_map/all_gather | solution.py:67
  8.0 328.1 %all-gather.10.cloned.1.call-start = ((), (), s32[]{:S(2)}) async-start(), calls=%async_computation.12 | async-start | bytes 3686400 | tf_op jit(solution)/shard_map/all_gather | solution.py:83
  31.7 247.7 %copy-start.30 = (f32[1600]{0:T(1024)}, f32[1600]{0:T(1024)S(1)}, u32[]{:S(2)}) copy-start(f32[1600]{0:T(1024)S(1)} %convert_element_type.230) | copy-start | bytes 19204
  31.8 247.5 %copy-start.32 = (f32[1600]{0:T(1024)}, f32[1600]{0:T(1024)S(1)}, u32[]{:S(2)}) copy-start(f32[1600]{0:T(1024)S(1)} %convert_element_type.231) | copy-start | bytes 19204
  32.1 247.3 %copy-start.35 = (f32[128]{0:T(128)}, f32[128]{0:T(128)S(1)}, u32[]{:S(2)}) copy-start(f32[128]{0:T(128)S(1)} %broadcast_multiply_fusion.2) | copy-start | bytes 1540
  32.8 246.5 %copy-start.37 = (f32[128]{0:T(128)}, f32[128]{0:T(128)S(1)}, u32[]{:S(2)}) copy-start(f32[128]{0:T(128)S(1)} %fusion.110) | copy-start | bytes 1540
  291.6 6.5 copy-start.41
  292.7 74.2 %all-gather.8.cloned.1.call-start = ((), (), s32[]{:S(2)}) async-start(), calls=%async_computation.11 | async-start | bytes 3686400 | tf_op jit(solution)/shard_map/all_gather | solution.py:84
  293.4 37.3 %collective-permute-start = (bf16[400,1600]{1,0:T(8,128)(2,1)S(1)}, bf16[400,1600]{1,0:T(8,128)(2,1)S(1)}, u32[]{:S(2)}, u32[]{:S(2)}) collective-permute-start(bf16[400,1600]{1,0:T(8,128)(2,1)S(1)} %copy-done.28), channel_id=1, source_target_pairs={{0,1},{1,0},{2,3},{3,2},{4,5},{5,4},{6,7},{7,6},{8,9},{9,8},{10,11... | collective-permute-start | bytes 3840008 | tf_op jit(solution)/shard_map/ppermute | solution.py:14
  294.2 30.7 %all-to-all-start = ((bf16[400,4,3]{0,2,1:T(4,128)(2,1)}), bf16[400,4,3]{0,2,1:T(4,128)(2,1)S(1)}, u32[]{:S(2)}, u32[]{:S(2)}) async-start(bf16[400,4,3]{0,2,1:T(4,128)(2,1)} %tile.2), calls=%async_computation | async-start | bytes 32768 | tf_op jit(solution)/shard_map/all_to_all | solution.py:139
  297.5 299.2 %all-gather.14.cloned.1.call-start = ((), (), s32[]{:S(2)}) async-start(), calls=%async_computation.14 | async-start | bytes 2048000 | tf_op jit(solution)/shard_map/all_gather | solution.py:147
  324.9 279.7 %all-to-all-start.1 = ((bf16[400,4,1600]{2,0,1:T(8,128)(2,1)}), bf16[400,4,1600]{2,0,1:T(8,128)(2,1)}, u32[]{:S(2)}, u32[]{:S(2)}) async-start(bf16[400,4,1600]{2,0,1:T(8,128)(2,1)} %copy.78), calls=%async_computation.1 | async-start | bytes 10649600 | tf_op jit(solution)/shard_map/all_to_all | solution.py:138
  329.9 304.6 %all-gather.12.cloned.1.call-start = ((), (), s32[]{:S(2)}) async-start(), calls=%async_computation.13 | async-start | bytes 2048000 | tf_op jit(solution)/shard_map/all_gather | solution.py:146
  333.2 254.1 %collective-permute-start.1 = (bf16[800,1600]{1,0:T(8,128)(2,1)}, bf16[800,1600]{1,0:T(8,128)(2,1)}, u32[]{:S(2)}, u32[]{:S(2)}) collective-permute-start(bf16[800,1600]{1,0:T(8,128)(2,1)} %maximum_select_fusion.1), channel_id=1, source_target_pairs={{0,2},{1,3},{2,0},{3,1},{4,6},{5,7},{6,4},{7,5},{8,10},{9,11},{10,... | collective-permute-start | bytes 7680008 | tf_op jit(solution)/shard_map/ppermute | solution.py:14
  391.8 202.6 %copy-start.17 = (bf16[128,25,64]{0,2,1:T(8,128)(2,1)}, bf16[128,25,64]{0,2,1:T(8,128)(2,1)S(1)}, u32[]{:S(2)}) copy-start(bf16[128,25,64]{0,2,1:T(8,128)(2,1)S(1)} %convert_element_type.234) | copy-start | bytes 1228804
  587.3 9.3 copy-start.39
  596.6 97.1 %reduce-scatter.21.cloned.1.call-start = ((), (), s32[]{:S(2)}) async-start(), calls=%async_computation.18 | async-start | bytes 2129920
  657.8 155.4 %reduce-scatter.25.cloned.1.call-start = ((), (), s32[]{:S(2)}) async-start(), calls=%async_computation.20 | async-start | bytes 3833856
  701.1 6.4 copy-start.25
  701.1 6.4 copy-start.16
  708.3 5.2 copy-start
  720.2 3.3 copy-start.3
  720.2 3.3 copy-start.11
  720.2 4.6 copy-start.14
  723.5 4.2 copy-start.2
  724.7 6.0 copy-start.12
  727.6 4.8 copy-start.1
  732.5 5.2 copy-start
  744.3 3.5 copy-start.3
  744.4 3.5 copy-start.11
  744.4 4.8 copy-start.14
  747.8 4.2 copy-start.2
  749.1 6.0 copy-start.12
  752.0 4.8 copy-start.1
  766.8 97.8 %reduce-scatter.23.cloned.1.call-start = ((), (), s32[]{:S(2)}) async-start(), calls=%async_computation.19 | async-start | bytes 3833856
  776.5 324.3 %reduce-scatter.17.cloned.1.call-start = ((), (), s32[]{:S(2)}) async-start(), calls=%async_computation.16 | async-start | bytes 6656000 | tf_op jit(solution)/shard_map/reduce_scatter | solution.py:288
  781.6 84.2 %copy-start.8 = (bf16[128,1600]{0,1:T(8,128)(2,1)S(1)}, bf16[128,1600]{0,1:T(8,128)(2,1)}, u32[]{:S(2)}) copy-start(bf16[128,1600]{0,1:T(8,128)(2,1)} %param.22) | copy-start | bytes 1228804
  781.6 84.2 %copy-start.31 = (f32[1600]{0:T(1024)S(1)}, f32[1600]{0:T(1024)}, u32[]{:S(2)}) copy-start(f32[1600]{0:T(1024)} %copy-done.30) | copy-start | bytes 19204
  781.6 84.3 %copy-start.33 = (f32[1600]{0:T(1024)S(1)}, f32[1600]{0:T(1024)}, u32[]{:S(2)}) copy-start(f32[1600]{0:T(1024)} %copy-done.32) | copy-start | bytes 19204
  781.7 84.3 %copy-start.36 = (f32[128]{0:T(128)S(1)}, f32[128]{0:T(128)}, u32[]{:S(2)}) copy-start(f32[128]{0:T(128)} %copy-done.35) | copy-start | bytes 1540
  781.7 84.3 %copy-start.38 = (f32[128]{0:T(128)S(1)}, f32[128]{0:T(128)}, u32[]{:S(2)}) copy-start(f32[128]{0:T(128)} %copy-done.37) | copy-start | bytes 1540
  781.7 547.0 %reduce-scatter.15.cloned.1.call-start = ((), (), s32[]{:S(2)}) async-start(), calls=%async_computation.15 | async-start | bytes 19456000 | tf_op jit(solution)/shard_map/reduce_scatter | solution.py:279
  783.1 91.8 %copy-start.22 = (bf16[128,25,64]{0,2,1:T(8,128)(2,1)}, bf16[128,25,64]{0,2,1:T(8,128)(2,1)S(1)}, u32[]{:S(2)}) copy-start(bf16[128,25,64]{0,2,1:T(8,128)(2,1)S(1)} %get-tuple-element.465) | copy-start | bytes 1228804
  814.5 60.4 %copy-start.23 = (bf16[128,1600]{0,1:T(8,128)(2,1)}, bf16[128,1600]{0,1:T(8,128)(2,1)S(1)}, u32[]{:S(2)}) copy-start(bf16[128,1600]{0,1:T(8,128)(2,1)S(1)} %copy.96) | copy-start | bytes 1228804
  865.9 9.0 copy-start.24
  882.6 201.4 %all-to-all-start.3 = ((bf16[4,400,1600]{2,1,0:T(8,128)(2,1)}), bf16[4,400,1600]{2,1,0:T(8,128)(2,1)}, u32[]{:S(2)}, u32[]{:S(2)}) async-start(bf16[4,400,1600]{2,1,0:T(8,128)(2,1)} %bitcast.209), calls=%async_computation.5 | async-start | bytes 10649600 | tf_op jit(solution)/shard_map/all_to_all | solution.py:190
  887.7 480.4 %reduce-scatter.19.cloned.1.call-start = ((), (), s32[]{:S(2)}) async-start(), calls=%async_computation.17 | async-start | bytes 2129920
  895.8 3.9 copy-start.21
  899.5 678.8 %all-reduce.16.cloned.1.call-start = ((), (), s32[]{:S(2)}) async-start(), calls=%async_computation.21 | async-start | bytes 31334400 | tf_op jit(solution)/shard_map/psum | solution.py:298
  1328.7 40.7 %copy-start.20 = (bf16[128,1600]{1,0:T(8,128)(2,1)S(1)}, bf16[128,1600]{1,0:T(8,128)(2,1)}, u32[]{:S(2)}) copy-start(bf16[128,1600]{1,0:T(8,128)(2,1)} %reduce-scatter.25.cloned.1.call-done) | copy-start | bytes 1228804
  1330.6 38.8 %all-to-all-start.2 = ((bf16[4,400,2]{1,2,0:T(2,128)(2,1)}), bf16[4,400,2]{1,2,0:T(2,128)(2,1)S(1)}, u32[]{:S(2)}, u32[]{:S(2)}) async-start(bf16[4,400,2]{1,2,0:T(2,128)(2,1)} %copy.83), calls=%async_computation.4 | async-start | bytes 16384 | tf_op jit(solution)/shard_map/all_to_all | solution.py:193
  1369.5 9.4 copy-start.52
  1369.5 27.3 %copy-start.40 = (bf16[1600]{0:T(1024)(128)(2,1)S(1)}, bf16[1600]{0:T(1024)(128)(2,1)}, u32[]{:S(2)}) copy-start(bf16[1600]{0:T(1024)(128)(2,1)} %get-tuple-element.460) | copy-start | bytes 9604
  1369.6 56.8 %copy-start.5 = (f32[128,1600]{0,1:T(8,128)S(1)}, f32[128,1600]{0,1:T(8,128)}, u32[]{:S(2)}) copy-start(f32[128,1600]{0,1:T(8,128)} %copy-done.4) | copy-start | bytes 2457604
  1369.6 56.8 %copy-start.9 = (bf16[128,1600]{0,1:T(8,128)(2,1)S(1)}, bf16[128,1600]{0,1:T(8,128)(2,1)}, u32[]{:S(2)}) copy-start(bf16[128,1600]{0,1:T(8,128)(2,1)} %copy.92) | copy-start | bytes 1228804
  1369.6 56.7 %copy-start.10 = (bf16[128,1600]{0,1:T(8,128)(2,1)S(1)}, bf16[128,1600]{0,1:T(8,128)(2,1)}, u32[]{:S(2)}) copy-start(bf16[128,1600]{0,1:T(8,128)(2,1)} %param.37) | copy-start | bytes 1228804
  1369.6 56.7 %copy-start.34 = (f32[1600]{0:T(1024)S(1)}, f32[1600]{0:T(1024)}, u32[]{:S(2)}) copy-start(f32[1600]{0:T(1024)} %get-tuple-element.378) | copy-start | bytes 19204
  1578.3 7.6 slice-start.2
  1578.3 6.0 copy-start.27
  1578.3 7.6 slice-start.3
  1584.2 6.4 slice-start
  1585.9 4.7 slice-start.1
  (21 other events, 33.2 us)
Sparse Core Ops, SparseCore 0:
  9.6 269.6 all-gather.5
  292.8 31.6 all-gather.9
  326.9 33.2 all-gather.7
  361.6 154.0 all-gather.13
  596.7 37.7 all-gather.11
  658.0 35.6 reduce-scatter.20
  766.9 46.2 reduce-scatter.24
  817.3 47.3 reduce-scatter.22
  867.5 164.1 reduce-scatter.16
  1034.0 294.6 reduce-scatter.14
  1331.6 36.5 reduce-scatter.18
  1372.6 205.6 all-reduce.15
